TPU v7x, 256 devices: a whole 4x4x8 slice. The times are simulated.
256 devices in a mesh: cand: 16 (over z_hi, x, core), seq: 16 (over z_lo, y).
Axes of the slice: x: 4, y: 4, z: 8 (z_hi: 2, z_lo: 4; z = z_hi * 4 + z_lo), core: 2. Of those that a mesh axis runs over, the one named last changes fastest.
Arguments:
- latent: bfloat16 [16, 768, 3072], P('cand', 'seq'), may hold values from -0.59765625 to 0.59765625
- timesteps: int32 [16], replicated, may hold values from 0 to 999
- positions: int32 [3, 768], replicated, may hold values from 0 to 63
- mod_weight: bfloat16 [3072, 9216], P('cand', 'seq'), may hold values from -0.109375 to 0.109375
- input_weight: bfloat16 [3072, 16, 384], P('cand', 'seq'), may hold values from -0.109375 to 0.109375
- output_weight: bfloat16 [16, 128, 3072], P('seq', None, 'cand'), may hold values from -0.75 to 0.75
- cotangent: bfloat16 [16, 768, 3072], P('cand', 'seq'), may hold values from -6 to 6
Outputs:
- block_out: bfloat16 [16, 768, 3072], P('cand', 'seq')
- latent_grad: float32 [16, 768, 3072], P('cand', 'seq')
All inputs are finite; a program needn't handle non-finite values.
Results may differ from a plain program's by a relative error of at most 0.033.
Values may be sent and summed in bfloat16 or wider, within the bound.
No kernel may reach another device: no remote copies, remote signals or barrier semaphores. Data moves between devices by JAX's collectives and lax.ppermute only.
A program may use at most 128 MiB of HBM per device.

v0:
```python
import jax
import jax.numpy as jnp
import numpy as np
from jax import lax
from jax.sharding import PartitionSpec as P

HEAD = 128
epsilon = 1e-06


def in_blocks(value, dim, size):
    dims = value.shape
    parts = value.reshape(*dims[:dim], size, dims[dim] // size, *dims[dim + 1 :])
    return jnp.moveaxis(parts, dim, 0)


def summed_on_arrival(value, axis, dim):
    size = lax.axis_size(axis)
    parts = lax.all_to_all(in_blocks(value, dim, size), axis, 0, 0, tiled=True)
    return jnp.sum(parts.astype(jnp.float32), axis=0)


def in_order(parts, dim):
    parts = jnp.moveaxis(parts, 0, dim)
    dims = parts.shape
    return parts.reshape(*dims[:dim], dims[dim] * dims[dim + 1], *dims[dim + 2 :])


def from_everyone(value, axis):
    copies = jnp.broadcast_to(value, (lax.axis_size(axis), *value.shape))
    return lax.all_to_all(copies, axis, split_axis=0, concat_axis=0, tiled=True)


def gathered_copies(value, axis, dim):
    return in_order(from_everyone(value, axis), dim)


def time_embed(timesteps, feature_width):
    half_size = feature_width // 2
    freq_rate = jnp.exp(-jnp.log(10000.0) * jnp.arange(half_size, dtype=jnp.float32) / half_size)
    angles = timesteps.astype(jnp.float32)[:, None] * freq_rate[None, :]
    return jnp.concatenate([jnp.cos(angles), jnp.sin(angles)], axis=1)


def rope_tables(positions, head_size):
    first_size = head_size // 8
    other_size = (head_size - first_size) // 2
    pieces = []
    swapped = []
    sign_vec = []
    offset = 0
    for axis_id, width_part in enumerate((first_size, other_size, other_size)):
        half_size = width_part // 2
        freq_rate = jnp.exp(
            -jnp.log(256.0) * 2.0 * jnp.arange(half_size, dtype=jnp.float32) / width_part
        )
        angle_part = positions[axis_id].astype(jnp.float32)[:, None] * freq_rate[None, :]
        pieces.append(angle_part)
        pieces.append(angle_part)
        swapped += list(range(offset + half_size, offset + width_part)) + list(
            range(offset, offset + half_size)
        )
        sign_vec += [-1.0] * half_size + [1.0] * half_size
        offset += width_part
    angles = jnp.concatenate(pieces, axis=1)
    return (
        jnp.cos(angles),
        jnp.sin(angles),
        np.array(swapped, np.int32),
        np.array(sign_vec, np.float32),
    )


def rotate(values, tables):
    cos_tab, sin_tab, swapped, sign_vec = tables
    return values * cos_tab + values[..., swapped] * sign_vec * sin_tab


def unrotate(values, tables):
    cos_tab, sin_tab, swapped, sign_vec = tables
    return values * cos_tab - (values * sin_tab)[..., swapped] * sign_vec


def rms_norm(values):
    inverse = lax.rsqrt(jnp.mean(values * values, -1, keepdims=True) + epsilon)
    return (values * inverse, inverse)


def rms_back(d_normed, normed, inverse):
    return inverse * (d_normed - normed * jnp.mean(d_normed * normed, -1, keepdims=True))


def layer_norm(values):
    centred = values - jnp.mean(values, -1, keepdims=True)
    inverse_std = lax.rsqrt(jnp.mean(centred * centred, -1, keepdims=True) + epsilon)
    return (centred * inverse_std, inverse_std)


def layer_norm_back(d_normed, normed, inverse_std):
    return inverse_std * (
        d_normed
        - jnp.mean(d_normed, -1, keepdims=True)
        - normed * jnp.mean(d_normed * normed, -1, keepdims=True)
    )


def times_transposed(left, right):
    return lax.dot_general(
        left, right, (((1,), (1,)), ((), ())), preferred_element_type=jnp.float32
    )


def attend(projected, tables):
    length, groups, triple = projected.shape
    head_size = triple // 3
    grouped = jnp.transpose(projected.reshape(length, groups, 3, head_size), (2, 1, 0, 3))
    query_n, query_inv = rms_norm(grouped[0])
    key_n, key_inv = rms_norm(grouped[1])
    q_rot = rotate(query_n, tables).astype(jnp.bfloat16)
    k_rot = rotate(key_n, tables).astype(jnp.bfloat16)
    values = grouped[2].astype(jnp.bfloat16)
    score_scale = head_size ** (-0.5)
    scores = (
        jnp.einsum("gld,gmd->glm", q_rot, k_rot, preferred_element_type=jnp.float32) * score_scale
    )
    weights = jnp.exp(scores - head_size**0.5)
    probs = weights / jnp.sum(weights, -1, keepdims=True)
    probs_low = probs.astype(jnp.bfloat16)
    heads_out = jnp.einsum("glm,gmd->gld", probs_low, values, preferred_element_type=jnp.float32)
    attended = (
        jnp.transpose(heads_out, (1, 0, 2)).reshape(length, groups * head_size).astype(jnp.bfloat16)
    )
    saved = (q_rot, k_rot, values, probs, probs_low, query_n, query_inv, key_n, key_inv)
    return (attended, saved)


def attend_back(d_attended, saved, tables):
    q_rot, k_rot, values, probs, probs_low, query_n, query_inv, key_n, key_inv = saved
    groups, length, head_size = q_rot.shape
    score_scale = head_size ** (-0.5)
    d_heads = jnp.transpose(d_attended.reshape(length, groups, head_size), (1, 0, 2))
    d_values = jnp.einsum("glm,gld->gmd", probs_low, d_heads, preferred_element_type=jnp.float32)
    d_probs = jnp.einsum("gld,gmd->glm", d_heads, values, preferred_element_type=jnp.float32)
    d_scores = (probs * (d_probs - jnp.sum(probs * d_probs, -1, keepdims=True))).astype(
        jnp.bfloat16
    )
    d_qrot = (
        jnp.einsum("glm,gmd->gld", d_scores, k_rot, preferred_element_type=jnp.float32)
        * score_scale
    )
    d_krot = (
        jnp.einsum("glm,gld->gmd", d_scores, q_rot, preferred_element_type=jnp.float32)
        * score_scale
    )
    d_query = rms_back(unrotate(d_qrot, tables), query_n, query_inv)
    d_key = rms_back(unrotate(d_krot, tables), key_n, key_inv)
    stacked = jnp.stack([d_query, d_key, d_values], 0)
    return (
        jnp.transpose(stacked, (2, 1, 0, 3))
        .reshape(length, groups * 3 * head_size)
        .astype(jnp.bfloat16)
    )


def on_device(latent, timesteps, positions, mod_weight, input_weight, output_weight, cotangent):
    width = latent.shape[2]
    rows_local = latent.shape[1]
    groups = input_weight.shape[1]
    group_cols = groups * input_weight.shape[2]
    time_act = jax.nn.silu(time_embed(timesteps, width)).astype(jnp.bfloat16)
    slab_rows = mod_weight.shape[0]
    act_rows = lax.dynamic_slice_in_dim(time_act, lax.axis_index("cand") * slab_rows, slab_rows, 1)
    mod_mine = summed_on_arrival(
        jnp.dot(act_rows, mod_weight, preferred_element_type=jnp.float32).astype(jnp.bfloat16),
        "cand",
        0,
    )
    modulation = gathered_copies(mod_mine, "seq", 1)[0]
    shift_vec = modulation[:width]
    scale_vec = modulation[width : 2 * width]
    gate_vec = modulation[2 * width :]
    latent_rows = latent[0].astype(jnp.float32)
    normed, inverse_std = layer_norm(latent_rows)
    modulated = (normed * (1.0 + scale_vec) + shift_vec).astype(jnp.bfloat16)
    gathered = lax.all_gather(modulated, "seq", axis=0, tiled=True)
    length = gathered.shape[0]
    tables = rope_tables(positions, HEAD)
    w_full = lax.all_gather(input_weight, "cand", axis=0, tiled=True).reshape(width, group_cols)
    projected = jnp.dot(gathered, w_full, preferred_element_type=jnp.float32)
    attended, saved = attend(projected.reshape(length, groups, 3 * HEAD), tables)
    w_heads = gathered_copies(output_weight, "seq", 0)
    w_all = lax.all_gather(w_heads, "cand", axis=2, tiled=True)
    w_all = w_all.reshape(w_all.shape[0] * w_all.shape[1], width)
    token_heads = lax.all_to_all(attended, "seq", split_axis=0, concat_axis=1, tiled=True)
    mixed = jnp.dot(token_heads, w_all, preferred_element_type=jnp.float32)
    block_out = (latent_rows + gate_vec * mixed).astype(jnp.bfloat16)
    d_mixed = (cotangent[0].astype(jnp.float32) * gate_vec).astype(jnp.bfloat16)
    d_tokens = times_transposed(d_mixed, w_all).astype(jnp.bfloat16)
    d_attended = lax.all_to_all(d_tokens, "seq", split_axis=1, concat_axis=0, tiled=True)
    d_projected = attend_back(d_attended, saved, tables)
    d_modulated = lax.psum_scatter(
        times_transposed(
            lax.slice_in_dim(d_projected, 0, rows_local * lax.axis_size("seq"), axis=0), w_full
        ).astype(jnp.bfloat16),
        "seq",
        scatter_dimension=0,
        tiled=True,
    ).astype(jnp.float32)
    latent_grad = cotangent[0].astype(jnp.float32) + layer_norm_back(
        d_modulated * (1.0 + scale_vec), normed, inverse_std
    )
    return (block_out[None], latent_grad[None])


def solution(mesh):
    placed = (
        P("cand", "seq", None),
        P(),
        P(),
        P("cand", "seq"),
        P("cand", "seq", None),
        P("seq", None, "cand"),
        P("cand", "seq", None),
    )
    return jax.shard_map(
        on_device,
        mesh=mesh,
        in_specs=placed,
        out_specs=(P("cand", "seq", None), P("cand", "seq", None)),
        check_vma=False,
    )
```

profile of v0, /device:TPU:4, one launch (start us, length us, event | category | flops | bytes accessed | tf_op | source)
XLA Modules:
  0.0 455.1 jit_solution(4602630234816793834)
XLA Ops:
  11.2 11.4 %all-to-all-start = ((bf16[16,2,288]{2,1,0:T(2,128)(2,1)}), bf16[16,2,288]{2,1,0:T(2,128)(2,1)S(1)}, u32[]{:S(2)}, u32[]{:S(2)}) async-start(bf16[16,2,288]{2,1,0:T(2,128)(2,1)} %reshape.1012), calls=%async_computation | async-start | bytes 49152 | tf_op jit(solution)/shard_map/all_to_all | solution.py:19
  23.7 1.2 fusion.46
  24.9 5.4 %all-to-all-done = bf16[16,2,288]{2,1,0:T(2,128)(2,1)S(1)} async-done(((bf16[16,2,288]{2,1,0:T(2,128)(2,1)}), bf16[16,2,288]{2,1,0:T(2,128)(2,1)S(1)}, u32[]{:S(2)}, u32[]{:S(2)}) %all-to-all-start) | async-done | bytes 18464 | tf_op jit(solution)/shard_map/all_to_all | solution.py:19
  31.2 6.0 %all-to-all-start.1 = ((f32[16,1,576]{2,1,0:T(1,128)}), f32[16,1,576]{2,1,0:T(1,128)S(1)}, u32[]{:S(2)}, u32[]{:S(2)}) async-start(f32[16,1,576]{2,1,0:T(1,128)} %broadcast_in_dim.16), calls=%async_computation.1 | async-start | bytes 81920 | tf_op jit(solution)/shard_map/all_to_all | solution.py:31
  37.3 8.1 %all-to-all-done.1 = f32[16,1,576]{2,1,0:T(1,128)S(1)} async-done(((f32[16,1,576]{2,1,0:T(1,128)}), f32[16,1,576]{2,1,0:T(1,128)S(1)}, u32[]{:S(2)}, u32[]{:S(2)}) %all-to-all-start.1) | async-done | bytes 36896 | tf_op jit(solution)/shard_map/all_to_all | solution.py:31
  45.6 1.9 fusion.40
  47.7 35.8 %all_to_all.44 = bf16[16,1,128,192]{2,3,1,0:T(8,128)(2,1)S(1)} all-to-all(bf16[16,1,128,192]{2,3,1,0:T(8,128)(2,1)S(1)} %broadcast_in_dim.19), channel_id=1, replica_groups=mesh['cand'=16,'seq'=16] {'seq'}, dimensions={0} | all-to-all | bytes 1572864 | tf_op jit(solution)/shard_map/all_to_all | solution.py:31
  83.6 1.4 copy.33
  86.0 1.4 fusion.82
  87.4 2.2 fusion.81
  89.6 4.3 copy.29
  93.9 79.1 %all-gather.5.cloned.1.call-done = bf16[768,3072]{1,0:T(8,128)(2,1)} async-done(((bf16[48,3072]{1,0:T(8,128)(2,1)}), bf16[768,3072]{1,0:T(8,128)(2,1)}) %all-gather.5.cloned.1.call-update) | async-done | bytes 4718608 | tf_op jit(solution)/shard_map/all_gather | solution.py:185
  173.0 5.1 %fusion.5 = f32[768,3,128]{0,2,1:T(8,128)S(1)} fusion(bf16[3,128,3072]{2,1,0:T(8,128)(2,1)} %bitcast.240, bf16[768,3072]{1,0:T(8,128)(2,1)} %all-gather.5.cloned.1.call-done), kind=kOutput, calls=%fused_computation.10 | convolution fusion | flops 1811939328 | bytes 8257536 | tf_op jit(solution)/shard_map/dot_general | solution.py:189
  179.2 1.6 gather_fusion
  180.7 132.4 %all-gather.9.cloned.1.call-done = bf16[16,1,128,3072]{2,0,1,3:T(8,128)(2,1)} async-done(((bf16[16,1,128,192]{2,0,1,3:T(8,128)(2,1)}), bf16[16,1,128,3072]{2,0,1,3:T(8,128)(2,1)}) %all-gather.9.cloned.1.call-update) | async-done | bytes 12582928 | tf_op jit(solution)/shard_map/all_gather | solution.py:192
  313.1 7.0 %fusion.28 = bf16[6,16,8,128]{3,2,1,0:T(8,128)(2,1)S(1)} fusion(bf16[384,8,16,128]{3,2,1,0:T(8,128)(2,1)} %bitcast.237, bf16[1,48,3072]{2,1,0:T(8,128)(2,1)S(1)} %copy-done.15, f32[3072]{0:T(1024)S(1)} %get-tuple-element.23), kind=kOutput, calls=%fused_computation.28 | convolution fusion | flops 604520448 | bytes 13086720 | tf_op jit(solution)/shard_map/dot_general | solution.py:108
  320.9 4.4 all-to-all-start.4
  326.4 2.0 fusion.27
  328.4 6.9 %all-to-all-done.4 = bf16[48,16,128]{2,0,1:T(8,128)(2,1)S(1)} async-done(((bf16[48,16,128]{2,0,1:T(8,128)(2,1)}), bf16[48,16,128]{2,0,1:T(8,128)(2,1)S(1)}, u32[]{:S(2)}, u32[]{:S(2)}) %all-to-all-start.4) | async-done | bytes 196640 | tf_op jit(solution)/shard_map/all_to_all | solution.py:199
  335.3 2.6 multiply_reduce_fusion
  341.3 1.6 gather_fusion.3
  342.8 1.6 gather_fusion.2
  344.4 1.7 multiply_reduce_fusion.2
  346.6 1.2 copy-done.9
  347.9 4.3 convolution_convert_fusion
  352.2 1.1 convolution_convert_fusion.2
  353.3 3.5 all-to-all-start.2
  356.9 17.0 %copy.34 = bf16[16,1,128,3072]{3,2,0,1:T(8,128)(2,1)} copy(bf16[16,1,128,3072]{2,0,1,3:T(8,128)(2,1)} %all-gather.9.cloned.1.call-done) | data formatting | bytes 25165824 | tf_op jit(solution)/shard_map/all_gather | solution.py:192
  373.8 6.6 %fusion.19 = bf16[1,48,3072]{2,1,0:T(8,128)(2,1)} fusion(bf16[16,1,128,3072]{3,2,0,1:T(8,128)(2,1)} %copy.34, bf16[1,48,3072]{2,1,0:T(8,128)(2,1)S(1)} %copy-done.1, f32[3072]{0:T(1024)S(1)} %get-tuple-element.23, bf16[16,48,128]{2,1,0:T(8,128)(2,1)S(1)} %all-to-all-done.2), kind=kOutput, calls=%fused_computation.16 | convolution fusion | flops 604569600 | bytes 13381632 | tf_op jit(solution)/shard_map/dot_general | solution.py:195
  380.5 64.8 %reduce-scatter.2.cloned.1.call-done = bf16[48,3072]{1,0:T(8,128)(2,1)} async-done(((bf16[768,3072]{1,0:T(8,128)(2,1)}), bf16[48,3072]{1,0:T(8,128)(2,1)}) %reduce-scatter.2.cloned.1.call-update) | async-done | bytes 294928 | tf_op jit(solution)/shard_map/reduce_scatter | solution.py:201
  445.3 1.2 fusion.48
  446.5 2.0 fusion.45
  (94 shorter events, 13.8 us)
Async XLA Ops:
  7.2 1.9 copy-start
  7.2 40.4 %copy-start.17 = (bf16[1,128,192]{1,2,0:T(8,128)(2,1)S(1)}, bf16[1,128,192]{1,2,0:T(8,128)(2,1)}, u32[]{:S(2)}) copy-start(bf16[1,128,192]{1,2,0:T(8,128)(2,1)} %param.18) | copy-start | bytes 147460
  7.2 82.4 %all-gather.7.cloned.1.call-start = ((), (), s32[]{:S(2)}) async-start(), calls=%async_computation.7 | async-start | bytes 2506752 | tf_op jit(solution)/shard_map/all_gather | solution.py:188
  11.2 19.2 %all-to-all-start = ((bf16[16,2,288]{2,1,0:T(2,128)(2,1)}), bf16[16,2,288]{2,1,0:T(2,128)(2,1)S(1)}, u32[]{:S(2)}, u32[]{:S(2)}) async-start(bf16[16,2,288]{2,1,0:T(2,128)(2,1)} %reshape.1012), calls=%async_computation | async-start | bytes 49152 | tf_op jit(solution)/shard_map/all_to_all | solution.py:19
  31.2 14.3 %all-to-all-start.1 = ((f32[16,1,576]{2,1,0:T(1,128)}), f32[16,1,576]{2,1,0:T(1,128)S(1)}, u32[]{:S(2)}, u32[]{:S(2)}) async-start(f32[16,1,576]{2,1,0:T(1,128)} %broadcast_in_dim.16), calls=%async_computation.1 | async-start | bytes 81920 | tf_op jit(solution)/shard_map/all_to_all | solution.py:31
  37.2 135.8 %all-gather.5.cloned.1.call-start = ((), (), s32[]{:S(2)}) async-start(), calls=%async_computation.6 | async-start | bytes 5013504 | tf_op jit(solution)/shard_map/all_gather | solution.py:185
  47.5 265.6 %all-gather.9.cloned.1.call-start = ((), (), s32[]{:S(2)}) async-start(), calls=%async_computation.9 | async-start | bytes 13369344 | tf_op jit(solution)/shard_map/all_gather | solution.py:192
  47.5 37.5 %copy-start.18 = (s32[3,768]{1,0:T(4,128)S(1)}, s32[3,768]{1,0:T(4,128)}, u32[]{:S(2)}) copy-start(s32[3,768]{1,0:T(4,128)} %param.15) | copy-start | bytes 27652
  83.6 2.4 copy-start.20
  179.1 134.0 %copy-start.15 = (bf16[1,48,3072]{2,1,0:T(8,128)(2,1)S(1)}, bf16[1,48,3072]{2,1,0:T(8,128)(2,1)}, u32[]{:S(2)}) copy-start(bf16[1,48,3072]{2,1,0:T(8,128)(2,1)} %param.19) | copy-start | bytes 884740
  313.1 12.4 %copy-start.13 = (f32[128,768]{1,0:T(8,128)S(1)}, f32[128,768]{1,0:T(8,128)}, u32[]{:S(2)}) copy-start(f32[128,768]{1,0:T(8,128)} %gather_fusion) | copy-start | bytes 1179652
  313.1 12.4 %copy-start.19 = (f32[128]{0:T(128)S(1)}, f32[128]{0:T(128)}, u32[]{:S(2)}) copy-start(f32[128]{0:T(128)} %constant.63.clone) | copy-start | bytes 1540
  320.9 14.4 %all-to-all-start.4 = ((bf16[48,16,128]{2,0,1:T(8,128)(2,1)}), bf16[48,16,128]{2,0,1:T(8,128)(2,1)S(1)}, u32[]{:S(2)}, u32[]{:S(2)}) async-start(bf16[48,16,128]{2,0,1:T(8,128)(2,1)} %bitcast.224), calls=%async_computation.4 | async-start | bytes 393216 | tf_op jit(solution)/shard_map/all_to_all | solution.py:199
  325.3 120.0 %reduce-scatter.2.cloned.1.call-start = ((), (), s32[]{:S(2)}) async-start(), calls=%async_computation.8 | async-start | bytes 5013504 | tf_op jit(solution)/shard_map/reduce_scatter | solution.py:201
  325.7 0.7 copy-start.10
  335.3 2.6 copy-start.2
  338.5 1.6 copy-start.11
  338.6 1.6 copy-start.12
  340.2 1.1 copy-start.3
  342.8 1.6 copy-start.4
  344.4 1.8 copy-start.5
  344.4 1.8 copy-start.6
  344.4 1.8 copy-start.7
  344.4 1.8 copy-start.8
  344.4 2.1 copy-start.14
  346.1 1.7 copy-start.9
  353.3 20.5 %all-to-all-start.2 = ((bf16[16,48,128]{2,1,0:T(8,128)(2,1)}), bf16[16,48,128]{2,1,0:T(8,128)(2,1)S(1)}, u32[]{:S(2)}, u32[]{:S(2)}) async-start(bf16[16,48,128]{2,1,0:T(8,128)(2,1)} %convolution_convert_fusion.2), calls=%async_computation.2 | async-start | bytes 393216 | tf_op jit(solution)/shard_map/all_to_all | solution.py:194
  356.9 17.0 %copy-start.1 = (bf16[1,48,3072]{2,1,0:T(8,128)(2,1)S(1)}, bf16[1,48,3072]{2,1,0:T(8,128)(2,1)}, u32[]{:S(2)}) copy-start(bf16[1,48,3072]{2,1,0:T(8,128)(2,1)} %param.13) | copy-start | bytes 884740
  373.8 72.7 %copy-start.16 = (bf16[1,48,3072]{2,1,0:T(8,128)(2,1)S(1)}, bf16[1,48,3072]{2,1,0:T(8,128)(2,1)}, u32[]{:S(2)}) copy-start(bf16[1,48,3072]{2,1,0:T(8,128)(2,1)} %param.19) | copy-start | bytes 884740
Sparse Core Ops, SparseCore 0:
  10.7 70.0 all-gather.6
  83.2 89.8 all-gather.4
  175.8 137.3 all-gather.8
  352.3 92.9 reduce-scatter.1
where the time goes:
time: 456 us; the launch traced here: 455 us
  waiting for transfers between devices  298 us (65%)
  local copies, waits for them, and re-layouts  37.4 us (8%)
  blocking collectives  35.8 us (8%)
  matrix products  31.7 us (7%)
  starting transfers between devices  25.7 us (6%)
  between operations  14.2 us (3%)
  other arithmetic  12.7 us (3%)
    all_gather x1, waiting for transfers between devices, on_device(): w_all = lax.all_gather(w_heads, 'cand', axis=2, tiled=True)  132 us
    all_gather x1, waiting for transfers between devices, on_device(): gathered = lax.all_gather(modulated, 'seq', axis=0, tiled=True)  79.1 us
    reduce_scatter x1, waiting for transfers between devices, on_device(): lax.psum_scatter(times_transposed(lax.slice_in_dim(d_projected, 0, rows_l...  64.8 us
    all_to_all x1, blocking collectives, from_everyone(): return lax.all_to_all(copies, axis, split_axis=0, concat_axis=0, tiled=True)  35.8 us
    all_gather x1, local copies, waits for them, and re-layouts, on_device(): w_all = lax.all_gather(w_heads, 'cand', axis=2, tiled=True)  17 us
    all_to_all x1, starting transfers between devices, summed_on_arrival(): parts = lax.all_to_all(in_blocks(value, dim, size), axis, 0, 0, tiled=True)  11.4 us
    dot_general x2, matrix products, times_transposed(): lax.dot_general(left, right, (((1,), (1,)), ((), ())), preferred_element_...  11.3 us
  transfers between devices with their start and end apart: 8, of which 6 were waited for; matrix products, arithmetic and copies ran while one was open for 12% of the time, Pallas kernels for 0%

commit v1 on v0

--- a/solution.py
+++ b/solution.py
@@ -3,9 +3,23 @@
 import numpy as np
 from jax import lax
 from jax.sharding import PartitionSpec as P
+from jax.lax import all_to_all, axis_size
 
 HEAD = 128
 epsilon = 1e-06
+
+
+def values_wrap(work_x, out_dim):
+    prior = jnp.concatenate(
+        all_to_all(
+            jnp.stack([work_x for _ in range(axis_size("seq"))], axis=0),
+            "seq",
+            split_axis=0,
+            concat_axis=0,
+        ),
+        axis=out_dim,
+    )
+    return prior
 
 
 def in_blocks(value, dim, size):
@@ -182,7 +196,7 @@
     latent_rows = latent[0].astype(jnp.float32)
     normed, inverse_std = layer_norm(latent_rows)
     modulated = (normed * (1.0 + scale_vec) + shift_vec).astype(jnp.bfloat16)
-    gathered = lax.all_gather(modulated, "seq", axis=0, tiled=True)
+    gathered = values_wrap(modulated, 0)
     length = gathered.shape[0]
     tables = rope_tables(positions, HEAD)
     w_full = lax.all_gather(input_weight, "cand", axis=0, tiled=True).reshape(width, group_cols)

time: 456 us -> 423 us (0.928)
  waiting for transfers between devices: 298 us -> 251 us
  starting transfers between devices: 25.7 us -> 42.5 us
    all_to_all x0 -> x1, waiting for transfers between devices: none -> 163 us  [values_wrap(): all_to_all(jnp.stack([work_x for _ in range(axis_size('seq'))], axis=0),...]
    all_gather x1, waiting for transfers between devices: 132 us -> 0.01 us  [on_device(): w_all = lax.all_gather(w_heads, 'cand', axis=2, tiled=True)]
    all_gather x1 -> x0, waiting for transfers between devices: 79.1 us -> none  [on_device(): gathered = lax.all_gather(modulated, 'seq', axis=0, tiled=True)]
    all_to_all x1, starting transfers between devices: 4.39 us -> 20.6 us  [on_device(): lax.all_to_all(d_tokens, 'seq', split_axis=1, concat_axis=0, tiled=True)]
    all_to_all x0 -> x1, starting transfers between devices: none -> 4.7 us  [values_wrap(): all_to_all(jnp.stack([work_x for _ in range(axis_size('seq'))], axis=0),...]
  transfers between devices with their start and end apart: 8 -> 8, of which waited for: 6 -> 5; matrix products, arithmetic and copies ran while one was open for 12% -> 13% of each run, Pallas kernels for 0% -> 0%
where the time goes in v1:
time: 423 us; the launch traced here: 421 us
  waiting for transfers between devices  251 us (59%)
  starting transfers between devices  42.5 us (10%)
  local copies, waits for them, and re-layouts  40.2 us (10%)
  blocking collectives  33.3 us (8%)
  matrix products  31.3 us (7%)
  between operations  14.2 us (3%)
  other arithmetic  8.42 us (2%)
    all_to_all x1, waiting for transfers between devices, values_wrap(): all_to_all(jnp.stack([work_x for _ in range(axis_size('seq'))], axis=0),...  163 us
    reduce_scatter x1, waiting for transfers between devices, on_device(): lax.psum_scatter(times_transposed(lax.slice_in_dim(d_projected, 0, rows_l...  63.3 us
    all_to_all x1, blocking collectives, from_everyone(): return lax.all_to_all(copies, axis, split_axis=0, concat_axis=0, tiled=True)  33.3 us
    all_to_all x1, starting transfers between devices, on_device(): lax.all_to_all(d_tokens, 'seq', split_axis=1, concat_axis=0, tiled=True)  20.6 us
    all_gather x1, local copies, waits for them, and re-layouts, on_device(): w_all = lax.all_gather(w_heads, 'cand', axis=2, tiled=True)  16.7 us
    dot_general x2, matrix products, times_transposed(): lax.dot_general(left, right, (((1,), (1,)), ((), ())), preferred_element_...  11.3 us
    all_to_all x1, starting transfers between devices, summed_on_arrival(): parts = lax.all_to_all(in_blocks(value, dim, size), axis, 0, 0, tiled=True)  8.75 us
    all_to_all x1, waiting for transfers between devices, summed_on_arrival(): parts = lax.all_to_all(in_blocks(value, dim, size), axis, 0, 0, tiled=True)  8.61 us
  transfers between devices with their start and end apart: 8, of which 5 were waited for; matrix products, arithmetic and copies ran while one was open for 13% of the time, Pallas kernels for 0%

profile of v1, /device:TPU:4, one launch (start us, length us, event | category | flops | bytes accessed | tf_op | source)
XLA Modules:
  0.0 420.9 jit_solution(5003429844576711342)
XLA Ops:
  8.9 33.3 %all_to_all.49 = bf16[16,1,128,192]{2,3,1,0:T(8,128)(2,1)S(1)} all-to-all(bf16[16,1,128,192]{2,3,1,0:T(8,128)(2,1)S(1)} %broadcast_in_dim.19), channel_id=1, replica_groups=mesh['cand'=16,'seq'=16] {'seq'}, dimensions={0} | all-to-all | bytes 1572864 | tf_op jit(solution)/shard_map/all_to_all | solution.py:45
  42.3 1.4 copy.33
  46.3 8.7 %all-to-all-start = ((bf16[16,2,288]{2,1,0:T(2,128)(2,1)}), bf16[16,2,288]{2,1,0:T(2,128)(2,1)S(1)}, u32[]{:S(2)}, u32[]{:S(2)}) async-start(bf16[16,2,288]{2,1,0:T(2,128)(2,1)} %reshape.1043), calls=%async_computation | async-start | bytes 49152 | tf_op jit(solution)/shard_map/all_to_all | solution.py:33
  55.5 8.6 %all-to-all-done = bf16[16,2,288]{2,1,0:T(2,128)(2,1)S(1)} async-done(((bf16[16,2,288]{2,1,0:T(2,128)(2,1)}), bf16[16,2,288]{2,1,0:T(2,128)(2,1)S(1)}, u32[]{:S(2)}, u32[]{:S(2)}) %all-to-all-start) | async-done | bytes 18464 | tf_op jit(solution)/shard_map/all_to_all | solution.py:33
  64.9 4.6 %all-to-all-start.1 = ((f32[16,1,576]{2,1,0:T(1,128)}), f32[16,1,576]{2,1,0:T(1,128)S(1)}, u32[]{:S(2)}, u32[]{:S(2)}) async-start(f32[16,1,576]{2,1,0:T(1,128)} %broadcast_in_dim.16), calls=%async_computation.1 | async-start | bytes 81920 | tf_op jit(solution)/shard_map/all_to_all | solution.py:45
  69.5 8.2 %all-to-all-done.1 = f32[16,1,576]{2,1,0:T(1,128)S(1)} async-done(((f32[16,1,576]{2,1,0:T(1,128)}), f32[16,1,576]{2,1,0:T(1,128)S(1)}, u32[]{:S(2)}, u32[]{:S(2)}) %all-to-all-start.1) | async-done | bytes 36896 | tf_op jit(solution)/shard_map/all_to_all | solution.py:45
  78.1 2.7 stack.17
  80.9 4.7 %all-to-all-start.2 = ((bf16[16,48,3072]{2,1,0:T(8,128)(2,1)}), bf16[16,48,3072]{2,1,0:T(8,128)(2,1)}, u32[]{:S(2)}, u32[]{:S(2)}) async-start(bf16[16,48,3072]{2,1,0:T(8,128)(2,1)} %stack.17), calls=%async_computation.2 | async-start | bytes 9437184 | tf_op jit(solution)/shard_map/all_to_all | solution.py:14
  86.6 1.4 fusion.82
  88.0 2.2 fusion.81
  90.2 4.4 %copy.29 = bf16[384,3072]{1,0:T(8,128)(2,1)} copy(bf16[384,3072]{0,1:T(8,128)(2,1)} %bitcast.236) | data formatting | bytes 4718592 | tf_op jit(solution)/shard_map/dot_general | solution.py:203
  94.6 163.1 %all-to-all-done.2 = bf16[16,48,3072]{2,1,0:T(8,128)(2,1)} async-done(((bf16[16,48,3072]{2,1,0:T(8,128)(2,1)}), bf16[16,48,3072]{2,1,0:T(8,128)(2,1)}, u32[]{:S(2)}, u32[]{:S(2)}) %all-to-all-start.2) | async-done | bytes 4718624 | tf_op jit(solution)/shard_map/all_to_all | solution.py:14
  257.6 5.4 %fusion.83 = f32[768,3,128]{0,2,1:T(8,128)S(1)} fusion(bf16[768,3072,1]{1,0,2:T(8,128)(2,1)} %bitcast.4, bf16[3,128,3072]{2,1,0:T(8,128)(2,1)} %bitcast.237), kind=kOutput, calls=%fused_computation.130 | convolution fusion | flops 1811939328 | bytes 8257536 | tf_op jit(solution)/shard_map/dot_general | solution.py:203
  264.0 1.6 gather_fusion
  265.6 7.0 %fusion.26 = bf16[6,16,8,128]{3,2,1,0:T(8,128)(2,1)S(1)} fusion(bf16[384,8,16,128]{3,2,1,0:T(8,128)(2,1)} %bitcast.234, bf16[1,48,3072]{2,1,0:T(8,128)(2,1)S(1)} %copy-done.16, f32[3072]{0:T(1024)S(1)} %get-tuple-element.23), kind=kOutput, calls=%fused_computation.26 | convolution fusion | flops 604520448 | bytes 13086720 | tf_op jit(solution)/shard_map/dot_general | solution.py:122
  273.3 20.6 %all-to-all-start.5 = ((bf16[48,16,128]{2,0,1:T(8,128)(2,1)}), bf16[48,16,128]{2,0,1:T(8,128)(2,1)S(1)}, u32[]{:S(2)}, u32[]{:S(2)}) async-start(bf16[48,16,128]{2,0,1:T(8,128)(2,1)} %bitcast.221), calls=%async_computation.5 | async-start | bytes 393216 | tf_op jit(solution)/shard_map/all_to_all | solution.py:213
  294.4 2.0 fusion.25
  296.4 7.0 %all-to-all-done.5 = bf16[48,16,128]{2,0,1:T(8,128)(2,1)S(1)} async-done(((bf16[48,16,128]{2,0,1:T(8,128)(2,1)}), bf16[48,16,128]{2,0,1:T(8,128)(2,1)S(1)}, u32[]{:S(2)}, u32[]{:S(2)}) %all-to-all-start.5) | async-done | bytes 196640 | tf_op jit(solution)/shard_map/all_to_all | solution.py:213
  303.4 2.6 multiply_reduce_fusion
  307.3 1.1 fusion.80
  308.4 1.6 gather_fusion.3
  310.0 1.6 gather_fusion.2
  311.5 1.7 multiply_reduce_fusion.2
  314.1 1.3 copy-done.11
  315.4 4.3 %convolution_convert_fusion = bf16[768,3072]{1,0:T(8,128)(2,1)} fusion(bf16[768,384]{0,1:T(8,128)(2,1)S(1)} %bitcast.240, bf16[3072,1,384]{2,0,1:T(8,128)(2,1)S(1)} %copy-done.11), kind=kOutput, calls=%fused_computation.9 | convolution fusion | flops 1814298624 | bytes 7667712 | tf_op jit(solution)/shard_map/dot_general | solution.py:122
  319.7 1.1 convolution_convert_fusion.2
  320.8 3.5 all-to-all-start.3
  324.4 16.7 %copy.34 = bf16[16,1,128,3072]{3,2,0,1:T(8,128)(2,1)} copy(bf16[16,1,128,3072]{2,0,1,3:T(8,128)(2,1)} %all-gather.6.cloned.1.call-done) | data formatting | bytes 25165824 | tf_op jit(solution)/shard_map/all_gather | solution.py:206
  341.1 6.7 %fusion.17 = bf16[1,48,3072]{2,1,0:T(8,128)(2,1)} fusion(bf16[16,1,128,3072]{3,2,0,1:T(8,128)(2,1)} %copy.34, bf16[1,48,3072]{2,1,0:T(8,128)(2,1)S(1)} %copy-done.3, f32[3072]{0:T(1024)S(1)} %get-tuple-element.23, bf16[16,48,128]{2,1,0:T(8,128)(2,1)S(1)} %all-to-all-done.3), kind=kOutput, calls=%fused_computation.14 | convolution fusion | flops 604569600 | bytes 13381632 | tf_op jit(solution)/shard_map/dot_general | solution.py:209
  347.8 63.3 %reduce-scatter.2.cloned.1.call-done = bf16[48,3072]{1,0:T(8,128)(2,1)} async-done(((bf16[768,3072]{1,0:T(8,128)(2,1)}), bf16[48,3072]{1,0:T(8,128)(2,1)}) %reduce-scatter.2.cloned.1.call-update) | async-done | bytes 294928 | tf_op jit(solution)/shard_map/reduce_scatter | solution.py:215
  411.1 1.2 fusion.47
  412.3 2.0 fusion.40
  (96 shorter events, 11.0 us)
Async XLA Ops:
  7.2 37.0 %copy-start = (bf16[192,576]{1,0:T(8,128)(2,1)S(1)}, bf16[192,576]{1,0:T(8,128)(2,1)}, u32[]{:S(2)}) copy-start(bf16[192,576]{1,0:T(8,128)(2,1)} %param.16) | copy-start | bytes 663556
  7.2 83.0 %all-gather.4.cloned.1.call-start = ((), (), s32[]{:S(2)}) async-start(), calls=%async_computation.7 | async-start | bytes 2506752 | tf_op jit(solution)/shard_map/all_gather | solution.py:202
  7.9 257.7 %all-gather.6.cloned.1.call-start = ((), (), s32[]{:S(2)}) async-start(), calls=%async_computation.9 | async-start | bytes 13369344 | tf_op jit(solution)/shard_map/all_gather | solution.py:206
  8.0 35.8 %copy-start.21 = (s32[16]{0:T(128)S(1)}, s32[16]{0:T(128)}, u32[]{:S(2)}) copy-start(s32[16]{0:T(128)} %param.14) | copy-start | bytes 196
  8.9 46.1 %copy-start.2 = (bf16[1,48,3072]{2,1,0:T(8,128)(2,1)S(1)}, bf16[1,48,3072]{2,1,0:T(8,128)(2,1)}, u32[]{:S(2)}) copy-start(bf16[1,48,3072]{2,1,0:T(8,128)(2,1)} %param.13) | copy-start | bytes 884740
  46.3 17.8 %all-to-all-start = ((bf16[16,2,288]{2,1,0:T(2,128)(2,1)}), bf16[16,2,288]{2,1,0:T(2,128)(2,1)S(1)}, u32[]{:S(2)}, u32[]{:S(2)}) async-start(bf16[16,2,288]{2,1,0:T(2,128)(2,1)} %reshape.1043), calls=%async_computation | async-start | bytes 49152 | tf_op jit(solution)/shard_map/all_to_all | solution.py:33
  64.9 12.8 %all-to-all-start.1 = ((f32[16,1,576]{2,1,0:T(1,128)}), f32[16,1,576]{2,1,0:T(1,128)S(1)}, u32[]{:S(2)}, u32[]{:S(2)}) async-start(f32[16,1,576]{2,1,0:T(1,128)} %broadcast_in_dim.16), calls=%async_computation.1 | async-start | bytes 81920 | tf_op jit(solution)/shard_map/all_to_all | solution.py:45
  80.8 4.7 %copy-start.18 = (s32[3,768]{1,0:T(4,128)S(1)}, s32[3,768]{1,0:T(4,128)}, u32[]{:S(2)}) copy-start(s32[3,768]{1,0:T(4,128)} %param.15) | copy-start | bytes 27652
  80.9 5.7 %copy-start.20 = (s32[128]{0:T(128)S(1)}, s32[128]{0:T(128)}, u32[]{:S(2)}) copy-start(s32[128]{0:T(128)} %constant.69) | copy-start | bytes 1540
  80.9 176.8 %all-to-all-start.2 = ((bf16[16,48,3072]{2,1,0:T(8,128)(2,1)}), bf16[16,48,3072]{2,1,0:T(8,128)(2,1)}, u32[]{:S(2)}, u32[]{:S(2)}) async-start(bf16[16,48,3072]{2,1,0:T(8,128)(2,1)} %stack.17), calls=%async_computation.2 | async-start | bytes 9437184 | tf_op jit(solution)/shard_map/all_to_all | solution.py:14
  264.0 1.6 copy-start.16
  265.6 28.6 %copy-start.13 = (f32[128,768]{1,0:T(8,128)S(1)}, f32[128,768]{1,0:T(8,128)}, u32[]{:S(2)}) copy-start(f32[128,768]{1,0:T(8,128)} %gather_fusion) | copy-start | bytes 1179652
  265.6 28.6 %copy-start.19 = (f32[128]{0:T(128)S(1)}, f32[128]{0:T(128)}, u32[]{:S(2)}) copy-start(f32[128]{0:T(128)} %constant.63.clone) | copy-start | bytes 1540
  273.3 30.1 %all-to-all-start.5 = ((bf16[48,16,128]{2,0,1:T(8,128)(2,1)}), bf16[48,16,128]{2,0,1:T(8,128)(2,1)S(1)}, u32[]{:S(2)}, u32[]{:S(2)}) async-start(bf16[48,16,128]{2,0,1:T(8,128)(2,1)} %bitcast.221), calls=%async_computation.5 | async-start | bytes 393216 | tf_op jit(solution)/shard_map/all_to_all | solution.py:213
  294.0 117.1 %reduce-scatter.2.cloned.1.call-start = ((), (), s32[]{:S(2)}) async-start(), calls=%async_computation.8 | async-start | bytes 5013504 | tf_op jit(solution)/shard_map/reduce_scatter | solution.py:215
  303.4 2.6 copy-start.14
  303.4 2.6 copy-start.4
  306.0 1.2 copy-start.12
  307.2 1.1 copy-start.5
  310.0 1.6 copy-start.6
  311.5 1.8 copy-start.15
  311.5 2.1 copy-start.7
  311.5 2.2 copy-start.8
  311.5 2.2 copy-start.9
  311.5 2.2 copy-start.10
  313.7 1.7 copy-start.11
  320.8 20.3 %all-to-all-start.3 = ((bf16[16,48,128]{2,1,0:T(8,128)(2,1)}), bf16[16,48,128]{2,1,0:T(8,128)(2,1)S(1)}, u32[]{:S(2)}, u32[]{:S(2)}) async-start(bf16[16,48,128]{2,1,0:T(8,128)(2,1)} %convolution_convert_fusion.2), calls=%async_computation.3 | async-start | bytes 393216 | tf_op jit(solution)/shard_map/all_to_all | solution.py:208
  324.4 16.8 %copy-start.3 = (bf16[1,48,3072]{2,1,0:T(8,128)(2,1)S(1)}, bf16[1,48,3072]{2,1,0:T(8,128)(2,1)}, u32[]{:S(2)}) copy-start(bf16[1,48,3072]{2,1,0:T(8,128)(2,1)} %param.13) | copy-start | bytes 884740
  341.1 71.2 %copy-start.17 = (bf16[1,48,3072]{2,1,0:T(8,128)(2,1)S(1)}, bf16[1,48,3072]{2,1,0:T(8,128)(2,1)}, u32[]{:S(2)}) copy-start(bf16[1,48,3072]{2,1,0:T(8,128)(2,1)} %param.19) | copy-start | bytes 884740
  341.1 73.2 %copy-start.1 = (bf16[192,576]{1,0:T(8,128)(2,1)S(1)}, bf16[192,576]{1,0:T(8,128)(2,1)}, u32[]{:S(2)}) copy-start(bf16[192,576]{1,0:T(8,128)(2,1)} %param.16) | copy-start | bytes 663556
Sparse Core Ops, SparseCore 0:
  10.7 67.6 all-gather.3
  81.2 179.5 all-gather.5
  319.8 91.2 reduce-scatter.1
